TPU v7x, 32 devices: a whole 2x2x4 slice. The times are simulated.
32 devices in a mesh: client: 16 (over z, y, core), tp: 2 (over x).
Axes of the slice: x: 2, y: 2, z: 4, core: 2. Of those that a mesh axis runs over, the one named last changes fastest.
Arguments:
- tokens: bfloat16 [4096, 2048], P('client'), may hold values from -6 to 6
- targets: bfloat16 [4096, 2048], P('client'), may hold values from -6 to 6
- norm_gain: float32 [2048], replicated, may hold values from 0.25 to 1.75
- up_frozen: bfloat16 [2048, 7168], P('client', 'tp'), may hold values from -0.125 to 0.125
- down_frozen: bfloat16 [7168, 2048], P('tp', 'client'), may hold values from -0.0625 to 0.0625
- up_left: float32 [16, 2048], replicated, may hold values from -1 to 1
- up_right: float32 [16, 7168], P(None, 'tp'), may hold values from -0.4375 to 0.4375
- down_left: float32 [16, 7168], P(None, 'tp'), may hold values from -0.625 to 0.625
- down_right: float32 [16, 2048], replicated, may hold values from -0.0625 to 0.0625
- counts: int32 [16], P('client'), may hold values from 64 to 4096
Outputs:
- round_up_left: float32 [16, 2048], replicated
- round_up_right: float32 [16, 7168], P(None, 'tp')
- round_down_left: float32 [16, 7168], P(None, 'tp')
- round_down_right: float32 [16, 2048], replicated
All inputs are finite; a program needn't handle non-finite values.
Results may differ from a plain program's by a relative error of at most 0.0089.
Values may be sent and summed in bfloat16 or wider, within the bound.
A program may use at most 128 MiB of HBM per device.

v0:
```python
import functools

import jax
import jax.numpy as jnp
from jax import lax
from jax.experimental import pallas as pl
from jax.experimental.pallas import tpu as pltpu
from jax.sharding import PartitionSpec as P

STEPS = 3
LEARN_RATE = 0.01
PROX_WEIGHT = 10.0
ADAPTER_SCALING = 0.5
NORM_EPS = 1e-05
LANES = 128

F32 = jnp.float32
BF16 = jnp.bfloat16
UNROLL = 7


def mm(a, b):
    return lax.dot_general(a, b, (((1,), (0,)), ((), ())), preferred_element_type=F32)


def mmt(a, b):
    return lax.dot_general(a, b, (((1,), (1,)), ((), ())), preferred_element_type=F32)


def update(value, grad, anchor):
    return value - LEARN_RATE * (grad + PROX_WEIGHT * (value - anchor))


def kernel(n, subs, bpa, bpb, tile, groups, up, dn, tokens, targets, gain, ul0h, ur0h, dl0h, dr0h, count,
           res,
           w0, w1, base, dact, gate, act, dpre, ptx, prx, dout, nx, diff,
           dnv, gainv, ul0, ur0, dl0, dr0,
           ul0p, dr0p, ulp, drp, ur, dl, ulb, drb, urb, dlb,
           lut, ldt, dldt, ldm, xtx, xrx, cntb,
           sbuf, abuf, bbuf, cbuf, rbuf,
           up_s, in_s, ring_s, ring_r, sib_s, sib_r, p_s, p_r, x_s, x_r, c_s, c_r,
           ab_s, ab_r, b_s, b_r, g_s, g_r, f_s, f_r, turn):
    R = n // 2
    half_ring = R // 2
    me = lax.axis_index("client")
    tp = lax.axis_index("tp")
    chip = me // 2
    core = me % 2
    sib = chip * 2 + (1 - core)
    ws = (w0, w1)
    rows, ffl = up.shape
    cr = 2 * rows
    half = rows // 2
    piece = half // subs
    tok = tokens.shape[0]
    rank = ul0.shape[0]
    n_tiles = ffl // tile

    low = chip % 2
    pos = jnp.where(low == 0, chip // 2, R - 1 - chip // 2)

    def chip_at(p):
        p = (p + 2 * R) % R
        return jnp.where(p < half_ring, 2 * p, 2 * (R - 1 - p) + 1)

    def slot_of(k, d):
        owner = k // 2
        at = owner // 2 if owner % 2 == 0 else R - 1 - owner // 2
        return (pos - at + R) % R if d == 0 else (at - pos + R) % R

    def lanes_of(k, d):
        return slice(d * rows + k % 2 * half, d * rows + k % 2 * half + half)

    def copy(src, dst, ss, rs, client, t):
        return pltpu.make_async_remote_copy(
            src_ref=src, dst_ref=dst, send_sem=ss, recv_sem=rs,
            device_id={"client": client, "tp": t},
            device_id_type=pl.DeviceIdType.MESH)

    nbr = (chip_at(pos + 1) * 2 + core, chip_at(pos - 1) * 2 + core)
    parts = [(d, u) for u in range(subs) for d in range(2)]

    def place(m, d, s, u, c):
        start = pl.multiple_of(d * rows + c * half + u * piece, piece)
        return ws[m].at[s, pl.ds(start, piece)]

    def ring_copy(m, d, s, u):
        return copy(place(m, d, s, u, core), place(m, d, s + 1, u, core),
                    ring_s.at[m, d, s, u], ring_r.at[m, d, s + 1, u], nbr[d], tp)

    def ring_arrived(m, d, s, u):
        ref = place(m, d, s, u, core)
        copy(ref, ref, ring_s.at[m, d, 0, u], ring_r.at[m, d, s, u], nbr[d], tp).wait_recv()

    def sib_copy(m, d, s, u, c):
        ref = place(m, d, s, u, c)
        return copy(ref, ref, sib_s.at[m, d, s, u], sib_r.at[m, d, s, u], sib, tp)

    def send_own(m):
        for d, u in parts:
            ring_copy(m, d, 0, u).start()
        for d, u in parts:
            sib_copy(m, d, 0, u, core).start()

    def advance(m, s, forward):
        for d, u in parts:
            ring_arrived(m, d, s, u)
            if forward:
                ring_copy(m, d, s, u).start()
            sib_copy(m, d, s, u, core).start()

    def sib_arrived(m, s):
        for d, u in parts:
            sib_copy(m, d, s, u, 1 - core).wait_recv()

    def tiles(fn, init=0, unroll=1):
        return lax.fori_loop(
            0, n_tiles, lambda i, c: fn(pl.ds(pl.multiple_of(i * tile, tile), tile), c), init,
            unroll=unroll)

    def each_slot(fn, lo=0, hi=None):
        hi = R if hi is None else hi
        if R <= 8:
            for s in range(lo, hi):
                fn(s)
        else:
            pl.loop(lo, hi)(fn)

    def slot_sum(fn, init):
        if R <= 8:
            for s in range(R):
                init = init + fn(s)
            return init
        return lax.fori_loop(0, R, lambda s, c: c + fn(s), init)

    width = tokens.shape[1]
    tokv = dpre.at[:, pl.ds(0, width)]
    tgtv = act.at[:, pl.ds(0, width)]
    ups = [pltpu.make_async_copy(up.at[pl.ds(d * half + u * piece, piece)], place(0, d, 0, u, core), up_s.at[d, u])
           for d, u in parts]
    ins = [pltpu.make_async_copy(a, b, in_s.at[i]) for i, (a, b) in enumerate((
        (tokens, tokv), (gain, gainv), (targets, tgtv), (ul0h, ul0), (ur0h, ur0),
        (dl0h, dl0), (dr0h, dr0), (dn, dnv)))]
    for c in ups:
        c.start()

    barrier = pltpu.get_barrier_semaphore()
    for client, t in ((nbr[0], tp), (nbr[1], tp), (sib, tp), (me, 1 - tp)):
        pl.semaphore_signal(barrier, inc=1, device_id={"client": client, "tp": t},
                            device_id_type=pl.DeviceIdType.MESH)
    pl.semaphore_wait(barrier, 4)

    for own in ups:
        own.wait()
    send_own(0)
    for c in ins:
        c.start()

    for c in ins:
        c.wait()
    strip = 64 if tok % 64 == 0 else tok

    @pl.loop(0, tok // strip)
    def _(i):
        here = pl.ds(pl.multiple_of(i * strip, strip), strip)
        wide = tokv[here, :].astype(F32)
        scale = lax.rsqrt(jnp.mean(wide * wide, axis=1, keepdims=True) + NORM_EPS)
        normed = (wide * scale * gainv[...]).astype(BF16)
        gap = wide - tgtv[here, :].astype(F32)
        for k in range(n):
            for d in range(2):
                at = slice(k * rows + d * half, k * rows + d * half + half)
                nx[slot_of(k, d), here, lanes_of(k, d)] = normed[:, at]
                diff[slot_of(k, d), here, lanes_of(k, d)] = gap[:, at]

    for k in range(n):
        for d in range(2):
            at = slice(k * rows + d * half, k * rows + d * half + half)
            for src, first in ((ul0, ul0p), (dr0, dr0p)):
                first[slot_of(k, d), :, lanes_of(k, d)] = src[:, at]
    for first, now, short in ((ul0p, ulp, ulb), (dr0p, drp, drb), (ur0, ur, urb), (dl0, dl, dlb)):
        now[...] = first[...]
        short[...] = first[...].astype(BF16)

    def turned(cols, c):
        flat = dnv[cols, :].T
        for d in range(2):
            w1[0, pl.ds(pl.multiple_of(d * rows + core * half, half), half), cols] = flat[d * half:(d + 1) * half]
        return c

    def add_base(s):
        sib_arrived(0, s)

        def body(cols, c):
            base[:, cols] += mm(nx[s], w0[s, :, cols])
            return c
        tiles(body)

    def first_base():
        sib_arrived(0, 0)

        def body(cols, c):
            base[:, cols] = mm(nx[0], w0[0, :, cols])
            return c
        tiles(body)

    def p_copy(s):
        return copy(ptx.at[s], prx.at[s], p_s.at[s], p_r.at[s], me, 1 - tp)

    def forward_piece(s):
        ptx[s] = mmt(act[...], w1[s]).astype(BF16)

    def output_piece(s):
        p_copy(s).wait_recv()
        total = ptx[s].astype(F32) + prx[s].astype(F32)
        out = diff[s] + total + ADAPTER_SCALING * mm(ldm[...], drb[s])
        grad = (out / tok).astype(BF16)
        dout[s] = grad
        dldt[...] += mmt(drb[s], grad)

    def through(s0, g, cols):
        if g == 1:
            return mm(dout[s0], w1[s0, :, cols])
        if cr % LANES:
            return sum(mm(dout[s0 + i], w1[s0 + i, :, cols]) for i in range(g))
        left = jnp.concatenate([dout[s0 + i] for i in range(g)], axis=1)
        return mm(left, w1[pl.ds(s0, g), :, cols].reshape(g * cr, tile))

    def backward(s0, g, first):
        def body(cols, c):
            d = through(s0, g, cols)
            dact[:, cols] = d if first else dact[:, cols] + d
            return c
        tiles(body, 0, UNROLL)

    def x_copy(k):
        return copy(xtx.at[k], xrx.at[k], x_s.at[k], x_r.at[k], me, 1 - tp)

    def begin_step():
        low_t = slot_sum(lambda s: mmt(ulb[s], nx[s]), jnp.zeros((rank, tok), F32))
        lut[...] = low_t.astype(BF16)
        lu = low_t.T.astype(BF16)

        def body(cols, c):
            pre = base[:, cols] + ADAPTER_SCALING * mm(lu, urb[:, cols])
            t = 0.5 * jnp.tanh(0.5 * pre)
            sig = 0.5 + t
            a = pre * sig
            ab = a.astype(BF16)
            act[:, cols] = ab
            gate[:, cols] = sig + a * (0.5 - t)
            return c + mmt(dlb[:, cols], ab)
        xtx[0] = tiles(body, jnp.zeros((rank, tok), F32), UNROLL)
        x_copy(0).start()
        dldt[...] = jnp.zeros_like(dldt)

    def take_low():
        x_copy(0).wait_recv()
        total = xtx[0] + xrx[0]
        ldt[...] = total.astype(BF16)
        ldm[...] = total.T.astype(BF16)

    def end_step(s0, g):
        dld = ADAPTER_SCALING * dldt[...]
        dld_t = dld.astype(BF16)
        dld_m = dld.T.astype(BF16)

        def body(cols, c):
            d = dact[:, cols] + through(s0, g, cols) + mm(dld_m, dlb[:, cols])
            h = (d * gate[:, cols]).astype(BF16)
            dpre[:, cols] = h
            return c + mmt(urb[:, cols], h)
        xtx[1] = ADAPTER_SCALING * tiles(body, jnp.zeros((rank, tok), F32), UNROLL)
        x_copy(1).start()

        def rest(cols, c):
            new = update(ur[:, cols], ADAPTER_SCALING * mm(lut[...], dpre[:, cols]), ur0[:, cols])
            ur[:, cols] = new
            urb[:, cols] = new.astype(BF16)
            new = update(dl[:, cols], mm(dld_t, act[:, cols]), dl0[:, cols])
            dl[:, cols] = new
            dlb[:, cols] = new.astype(BF16)
            return c
        tiles(rest, 0, UNROLL)

        def right(s):
            new = update(drp[s], ADAPTER_SCALING * mm(ldt[...], dout[s]), dr0p[s])
            drp[s] = new
            drb[s] = new.astype(BF16)
        each_slot(right)

    def end_left():
        x_copy(1).wait_recv()
        dlu_t = (xtx[1] + xrx[1]).astype(BF16)

        def left(s):
            new = update(ulp[s], mm(dlu_t, nx[s]), ul0p[s])
            ulp[s] = new
            ulb[s] = new.astype(BF16)
        each_slot(left)
        x_copy(0).wait_send()
        x_copy(1).wait_send()

        @pl.loop(0, R)
        def _(s):
            p_copy(s).wait_send()

    first_base()

    @pl.loop(1, R - 1)
    def _(s):
        advance(0, s, True)

        @pl.when(s == 1)
        def _():
            tiles(turned)

        @pl.when(s > 1)
        def _():
            add_base(s - 1)
    send_own(1)
    advance(0, R - 1, False)
    if R > 2:
        add_base(R - 2)
    add_base(R - 1)

    weight = count[0].astype(F32)
    cntb[me] = jnp.full(cntb.shape[1:], weight, F32)

    def cnt_copy(k):
        return copy(cntb.at[me], cntb.at[me], c_s.at[k], c_r.at[me], k, tp)

    @pl.loop(1, n)
    def _(i):
        cnt_copy((me + i) % n).start()
    advance(1, 1, R > 2)
    def pack(b, i0, per, change):
        owner, i = divmod(b, per)
        c, k = divmod(owner, R)
        sbuf[c, k, i0 + i] = (weight * change).astype(BF16)

    def wide_block(anchor, value, at):
        bits = []
        for lo in range(at, at + LANES, half):
            k, d = lo // rows, lo % rows // half
            where = (slot_of(k, d), slice(None), lanes_of(k, d))
            bits.append(anchor[where] - value[where])
        return jnp.concatenate(bits, axis=1)

    d = R * cr
    spans = (pl.ds(0, bpa), pl.ds(bpa, bpb))

    def pair(q):
        return copy(sbuf.at[1 - core, :, spans[q]], abuf.at[:, spans[q]], ab_s.at[q], ab_r.at[q], sib, tp)
    def chip_copy(q, k):
        return copy(bbuf.at[k, spans[q]], cbuf.at[chip, spans[q]], b_s.at[q, k], b_r.at[q, chip], k * 2 + core, tp)

    def chip_arrived(q, k):
        copy(bbuf.at[k, spans[q]], cbuf.at[k, spans[q]], b_s.at[q, k], b_r.at[q, k], k * 2 + core, tp).wait_recv()

    def back_copy(q, k):
        ref = rbuf.at[core, chip, spans[q]]
        return copy(ref, ref, g_s.at[q, k], g_r.at[q, chip], k * 2 + core, tp)

    def back_arrived(q, k):
        ref = rbuf.at[core, k, spans[q]]
        copy(ref, ref, g_s.at[q, k], g_r.at[q, k], k * 2 + core, tp).wait_recv()

    def pass_copy(q, c, k):
        ref = rbuf.at[c, k, spans[q]]
        return copy(ref, ref, f_s.at[q, k], f_r.at[q, k], sib, tp)

    def to_chips(q):
        pair(q).wait_recv()

        @pl.loop(0, R)
        def _(i):
            k = (chip + 1 + i) % R
            bbuf[k, spans[q]] = (sbuf[core, k, spans[q]].astype(F32) + abuf[k, spans[q]].astype(F32)).astype(BF16)

            @pl.when(i < R - 1)
            def _():
                chip_copy(q, k).start()
        cbuf[chip, spans[q]] = bbuf[chip, spans[q]]

    def last_sums():
        b = 0
        for value, anchor in ((ur, ur0), (dl, dl0)):
            for at in range(0, ffl, LANES):
                pack(b, 0, bpa, anchor[:, at:at + LANES] - value[:, at:at + LANES])
                b += 1

        for at in range(0, d, LANES):
            pack(b, 0, bpa, wide_block(dr0p, drp, at))
            b += 1
        for b in range(b, n * bpa):
            pack(b, 0, bpa, jnp.zeros(sbuf.shape[3:], F32))
        pair(0).start()

        to_chips(0)


    def gather_middle():
        sib_arrived(1, 0)
        forward_piece(0)
        p_copy(0).start()
        take_low()

        @pl.loop(2, R + 1)
        def _(s):
            @pl.when(s < R - 1)
            def _():
                advance(1, s, True)

            @pl.when(s == R - 1)
            def _():
                advance(1, s, False)
            sib_arrived(1, s - 1)
            forward_piece(s - 1)
            p_copy(s - 1).start()
            output_piece(s - 2)

            @pl.when(s == 2)
            def _():
                backward(0, 1, True)

            @pl.when(s > 2)
            def _():
                backward(s - 2, 1, False)
        output_piece(R - 1)

    def middle(t):
        held = t == 1

        @pl.loop(0, R)
        def _(s):
            forward_piece(s)

            @pl.when(jnp.logical_not(held & (core == 1)))
            def _():
                p_copy(s).start()

        @pl.when(held & (core == 1))
        def _():
            pl.semaphore_wait(turn, 1)

            @pl.loop(0, R)
            def _(s):
                p_copy(s).start()
        take_low()
        s0 = 0
        for g in groups:
            @pl.loop(s0, s0 + g)
            def _(s):
                output_piece(s)
            if s0 + g < R:
                backward(s0, g, s0 == 0)
            if s0 == 0:
                @pl.when(held & (core == 0))
                def _():
                    pl.semaphore_signal(turn, inc=1, device_id={"client": sib, "tp": tp},
                                        device_id_type=pl.DeviceIdType.MESH)
            s0 += g

    def step(t):
        begin_step()
        pl.when(t == 0)(gather_middle)
        pl.when(t > 0)(functools.partial(middle, t))
        end_step(R - 1, 1)

    @pl.loop(0, STEPS)
    def _(t):
        step(t)
        pl.when(t == STEPS - 1)(last_sums)
        end_left()

    b = 0
    for at in range(0, d, LANES):
        pack(b, bpa, bpb, wide_block(ul0p, ulp, at))
        b += 1
    for b in range(b, n * bpb):
        pack(b, bpa, bpb, jnp.zeros(sbuf.shape[3:], F32))
    pair(1).start()

    @pl.loop(1, n)
    def _(i):
        k = (me + i) % n
        copy(cntb.at[k], cntb.at[k], c_s.at[k], c_r.at[k], k, tp).wait_recv()
    total = lax.fori_loop(0, n, lambda k, c: c + cntb[k], jnp.zeros(cntb.shape[1:], F32))
    factor = LEARN_RATE * total[0:1, 0:1]
    to_chips(1)
    for q in range(2):
        @pl.loop(1, R)
        def _(i):
            chip_arrived(q, (chip + i) % R)
        s = lax.fori_loop(0, R, lambda k, c: c + cbuf[k, spans[q]].astype(F32),
                          jnp.zeros((spans[q].size,) + cbuf.shape[2:], F32))
        rbuf[core, chip, spans[q]] = (s / factor).astype(BF16)

        @pl.loop(1, R)
        def _(i):
            back_copy(q, (chip + i) % R).start()
        pass_copy(q, core, chip).start()
    for q in range(2):
        @pl.loop(1, R)
        def _(i):
            k = (chip + i) % R
            back_arrived(q, k)
            pass_copy(q, core, k).start()
    for q in range(2):
        @pl.loop(0, R)
        def _(k):
            pass_copy(q, 1 - core, k).wait_recv()
    res[...] = rbuf[...]

    for q in range(2):
        pair(q).wait_send()

        @pl.loop(1, R)
        def _(i):
            k = (chip + i) % R
            chip_copy(q, k).wait_send()
            back_copy(q, k).wait_send()

        @pl.loop(0, R)
        def _(k):
            pass_copy(q, core, k).wait_send()

    @pl.loop(1, n)
    def _(i):
        cnt_copy((me + i) % n).wait_send()
    for m in range(2):
        for d, u in parts:
            @pl.loop(0, R)
            def _(s):
                sib_copy(m, d, s, u, core).wait_send()

            @pl.loop(0, R - 1)
            def _(s):
                ring_copy(m, d, s, u).wait_send()


def spread(n, bpa, bpb, res, oul, our, odl, odr):
    R = n // 2

    def take(b, i0, per, out, at):
        owner, i = divmod(b, per)
        c, k = divmod(owner, R)
        out[:, at:at + LANES] = res[c, k, i0 + i].astype(F32)
    b = 0
    for out in (our, odl, odr):
        for at in range(0, out.shape[1], LANES):
            take(b, 0, bpa, out, at)
            b += 1
    for b, at in enumerate(range(0, oul.shape[1], LANES)):
        take(b, bpa, bpb, oul, at)


def per_device(n, tokens, targets, norm_gain, up_frozen, down_frozen,
               up_left, up_right, down_left, down_right, counts):
    R = n // 2
    tok, d = tokens.shape
    rank = up_left.shape[0]
    rows, ffl = up_frozen.shape
    cr = 2 * rows
    subs = 2 if rows % 64 == 0 else 1
    tile = 512 if ffl % 512 == 0 else 128
    groups, left = [], R
    while left > 1:
        groups.append(min(4, left // 2))
        left -= groups[-1]
    groups.append(1)
    bpa = -(-(2 * ffl + d) // (LANES * n))
    bpb = -(-d // (LANES * n))
    bpd = bpa + bpb
    vm = pl.BlockSpec(memory_space=pltpu.VMEM)
    sm = pl.BlockSpec(memory_space=pltpu.SMEM)
    hbm = pl.BlockSpec(memory_space=pl.ANY)
    V = pltpu.VMEM
    dma = lambda *s: pltpu.SemaphoreType.DMA(s)
    packed = pl.pallas_call(
        functools.partial(kernel, n, subs, bpa, bpb, tile, tuple(groups)),
        out_shape=jax.ShapeDtypeStruct((2, R, bpd, rank, LANES), BF16),
        in_specs=[hbm] * 9 + [sm],
        out_specs=vm,
        scratch_shapes=[
            V((R, cr, ffl), BF16), V((R, cr, ffl), BF16),
            V((tok, ffl), F32), V((tok, ffl), F32), V((tok, ffl), F32),
            V((tok, ffl), BF16), V((tok, ffl), BF16),
            V((R, tok, cr), BF16), V((R, tok, cr), BF16), V((R, tok, cr), BF16),
            V((R, tok, cr), BF16), V((R, tok, cr), F32),
            V((ffl, rows), BF16), V((1, d), F32),
            V((rank, d), F32), V((rank, ffl), F32), V((rank, ffl), F32), V((rank, d), F32),
            V((R, rank, cr), F32), V((R, rank, cr), F32), V((R, rank, cr), F32), V((R, rank, cr), F32),
            V((rank, ffl), F32), V((rank, ffl), F32),
            V((R, rank, cr), BF16), V((R, rank, cr), BF16), V((rank, ffl), BF16), V((rank, ffl), BF16),
            V((rank, tok), BF16), V((rank, tok), BF16), V((rank, tok), F32), V((tok, rank), BF16),
            V((2, rank, tok), F32), V((2, rank, tok), F32), V((n, 8, LANES), F32),
            V((2, R, bpd, rank, LANES), BF16), V((R, bpd, rank, LANES), BF16),
            V((R, bpd, rank, LANES), BF16), V((R, bpd, rank, LANES), BF16),
            V((2, R, bpd, rank, LANES), BF16),
            dma(2, subs), dma(8), dma(2, 2, R, subs), dma(2, 2, R, subs), dma(2, 2, R, subs), dma(2, 2, R, subs),
            dma(R), dma(R), dma(2), dma(2), dma(n), dma(n),
            dma(2), dma(2), dma(2, R), dma(2, R), dma(2, R), dma(2, R), dma(2, R), dma(2, R),
            pltpu.SemaphoreType.REGULAR,
        ],
        compiler_params=pltpu.CompilerParams(
            vmem_limit_bytes=65400 * 1024, has_side_effects=True, collective_id=0),
    )(up_frozen, down_frozen, tokens, targets, norm_gain.reshape(1, d),
      up_left, up_right, down_left, down_right, counts)
    return pl.pallas_call(
        functools.partial(spread, n, bpa, bpb),
        out_shape=[jax.ShapeDtypeStruct(a.shape, F32)
                   for a in (up_left, up_right, down_left, down_right)],
        in_specs=[vm],
        out_specs=[vm] * 4,
    )(packed)


def solution(mesh):
    placed = (
        P("client", None),
        P("client", None),
        P(),
        P("client", "tp"),
        P("tp", "client"),
        P(),
        P(None, "tp"),
        P(None, "tp"),
        P(),
        P("client"),
    )
    return jax.shard_map(
        functools.partial(per_device, mesh.shape["client"]),
        mesh=mesh,
        in_specs=placed,
        out_specs=(P(), P(None, "tp"), P(None, "tp"), P()),
        check_vma=False,
    )
```

profile of v0, /device:TPU:1, one launch (start us, length us, event | category | flops | bytes accessed | tf_op | source)
XLA Modules:
  0.0 235.8 jit_solution(3278870116038636152)
XLA Ops:
  1.3 232.6 %shard_map.129.res = bf16[2,8,6,16,128]{4,3,2,1,0:T(8,128)(2,1)} custom-call(bf16[128,3584]{1,0:T(8,128)(2,1)} %up.1, bf16[3584,128]{1,0:T(8,128)(2,1)} %dn.1, bf16[256,2048]{1,0:T(8,128)(2,1)} %tokens.1, bf16[256,2048]{1,0:T(8,128)(2,1)} %targets.1, f32[1,2048]{1,0:T(1,128)} %bitcast.1, f32[16,2048]{1,0:T(8,128)} %ul0h.1, f32[16,3584]{1,0:T(8,128)} %ur0h.1, ...), custom_call_target="tpu_custom_call" | custom-call | tf_op jit(solution)/shard_map/pallas_call | solution.py:581
  233.9 1.9 shard_map.130
where the time goes:
time: 236 us
  Pallas kernels  235 us (100%)
    pallas_call x1, Pallas kernels, per_device(): pl.pallas_call(functools.partial(kernel, n, subs, bpa, bpb, tile, tuple(g...  233 us

commit v1 on v0

--- a/solution.py
+++ b/solution.py
@@ -150,9 +150,11 @@
                             device_id_type=pl.DeviceIdType.MESH)
     pl.semaphore_wait(barrier, 4)
 
-    for own in ups:
+    for own, (d, u) in zip(ups, parts):
         own.wait()
-    send_own(0)
+        ring_copy(0, d, 0, u).start()
+    for d, u in parts:
+        sib_copy(0, d, 0, u, core).start()
     for c in ins:
         c.start()
 
@@ -455,7 +457,7 @@
                 output_piece(s)
             if s0 + g < R:
                 backward(s0, g, s0 == 0)
-            if s0 == 0:
+            if s0 == groups[0]:
                 @pl.when(held & (core == 0))
                 def _():
                     pl.semaphore_signal(turn, inc=1, device_id={"client": sib, "tp": tp},

time: 236 us -> 235 us (level)
  no operation moved by 1% of the time
where the time goes in v1:
time: 235 us
  Pallas kernels  234 us (100%)
    pallas_call x1, Pallas kernels, per_device(): pl.pallas_call(functools.partial(kernel, n, subs, bpa, bpb, tile, tuple(g...  232 us

profile of v1, /device:TPU:1, one launch (start us, length us, event | category | flops | bytes accessed | tf_op | source)
XLA Modules:
  0.0 235.1 jit_solution(3303331719803377339)
XLA Ops:
  1.3 231.9 %shard_map.129.res = bf16[2,8,6,16,128]{4,3,2,1,0:T(8,128)(2,1)} custom-call(bf16[128,3584]{1,0:T(8,128)(2,1)} %up.1, bf16[3584,128]{1,0:T(8,128)(2,1)} %dn.1, bf16[256,2048]{1,0:T(8,128)(2,1)} %tokens.1, bf16[256,2048]{1,0:T(8,128)(2,1)} %targets.1, f32[1,2048]{1,0:T(1,128)} %bitcast.1, f32[16,2048]{1,0:T(8,128)} %ul0h.1, f32[16,3584]{1,0:T(8,128)} %ur0h.1, ...), custom_call_target="tpu_custom_call" | custom-call | tf_op jit(solution)/shard_map/pallas_call | solution.py:583
  233.2 1.9 shard_map.130
